TPU v7x, 32 devices: a whole 2x2x4 slice. The times are simulated.
32 devices in a mesh: rec: 8 (over z, y), vocab: 4 (over x, core).
Axes of the slice: x: 2, y: 2, z: 4, core: 2. Of those that a mesh axis runs over, the one named last changes fastest.
Arguments:
- features: bfloat16 [32, 192, 1280], P('rec'), may hold values from -1000 to 1000
- head_weight: bfloat16 [1280, 32768], P(None, ('vocab', 'rec')), may hold values from -0.15625 to 0.15625
- labels: int32 [32, 128], P('rec'), may hold values from 0 to 32767
- audio_len: int32 [32], P(('rec', 'vocab')), may hold values from 1 to 192, as said below
- transcript_len: int32 [32], P(('rec', 'vocab')), may hold values from 1 to 128
Outputs:
- label_logprob: float32 [32, 192, 128], P(('rec', 'vocab'))
- path_score: float32 [32], P(('rec', 'vocab'))
Inputs may be any that keep to these rules, and one draw needn't show every extreme that they name: `audio_len`: each recording has at least as many frames in use as its transcript has labels.
All inputs are finite; a program needn't handle non-finite values.
Results may differ from a plain program's by a relative error of at most 0.00055.
Values may be sent and summed in bfloat16 or wider, within the bound.
A program may use at most 128 MiB of HBM per device.

v0:
```python
import functools
import jax
import jax.numpy as jnp
from jax import lax
from jax.experimental import pallas as pl
from jax.experimental.pallas import tpu as pltpu
from jax.sharding import PartitionSpec as P

MESH = pl.DeviceIdType.MESH
NEG = -1e30
run = 6


def flip(v, bit):
    return v + bit * (1 - 2 * ((v // bit) % 2))


def flip_mask(v, mask, bits):
    for bit in bits:
        if mask & bit:
            v = flip(v, bit)
    return v


def gather_kernel(a, b, V, x, w, lab, xo, wo, lo, sw, rw, sl, rl, sf, rf, sg, loc):
    r = lax.axis_index("rec")
    v = lax.axis_index("vocab")
    m, k = r // a, r % a
    own = x.shape[0] // V
    bits = []
    bit = V // 2
    while bit >= 1:
        bits.append(bit)
        bit //= 2
    col_peer = lambda d: (m * a + (k + d) % a, v)
    row_peer = lambda d: (((m + d) % b) * a + k, v)
    barrier = pltpu.get_barrier_semaphore()
    peers = [col_peer(d) for d in range(1, a)] + [row_peer(d) for d in range(1, b)]
    peers += [(r, flip(v, bit)) for bit in bits]
    for peer in peers:
        pl.semaphore_signal(barrier, inc=1, device_id=peer, device_id_type=MESH)
    pl.semaphore_wait(barrier, len(peers))

    def remote(src, dst, ss, rs, to):
        return pltpu.make_async_remote_copy(
            src_ref=src, dst_ref=dst, send_sem=ss, recv_sem=rs, device_id=to, device_id_type=MESH
        )

    sent = []

    def launch(*args):
        c = remote(*args)
        c.start()
        sent.append(c)

    piece = lambda ref, c: ref.at[pl.ds(c * own, own)]
    for d in range(1, b):
        launch(piece(x, v), piece(xo.at[m], v), sf.at[d - 1], rf.at[d - 1, 0], row_peer(d))
    for d in range(1, a):
        launch(w, wo.at[k], sw.at[d - 1], rw.at[d - 1], col_peer(d))
    for d in range(1, b):
        launch(lab, lo.at[m], sl.at[d - 1], rl.at[d - 1], row_peer(d))
    local = [
        pltpu.make_async_copy(x, xo.at[m], loc.at[0]),
        pltpu.make_async_copy(w, wo.at[k], loc.at[1]),
        pltpu.make_async_copy(lab, lo.at[m], loc.at[2]),
    ]
    for c in local:
        c.start()
    order = [0]
    for bit in bits:
        order += [mask | bit for mask in order]
    used = 0
    for mask in order:
        low = (mask & -mask) if mask else V
        c = flip_mask(v, mask, bits)
        for d in range(1, b):
            ms = (m + b - d) % b
            src = piece(xo.at[ms], c)
            remote(src, src, sf.at[d - 1], rf.at[d - 1, mask], row_peer(d)).wait_recv()
            for bit in bits:
                if bit < low:
                    launch(src, src, sg.at[used], rf.at[d - 1, mask | bit], (r, flip(v, bit)))
                    used += 1
    for d in range(1, a):
        ks = (k + a - d) % a
        remote(w, wo.at[ks], sw.at[d - 1], rw.at[d - 1], col_peer(d)).wait_recv()
    for d in range(1, b):
        ms = (m + b - d) % b
        remote(lab, lo.at[ms], sl.at[d - 1], rl.at[d - 1], row_peer(d)).wait_recv()
    for c in sent:
        c.wait_send()
    for c in local:
        c.wait()


def score_kernel(recs, tile, base_ref, x_ref, w_ref, lab_ref, pick_ref, stat_ref, logit):
    a, depth, cols = w_ref.shape
    frames = x_ref.shape[1]
    rows = recs * frames
    xs = x_ref[...].reshape(rows, depth)
    part = None
    acc = [None] * recs
    slots = lab_ref.shape[2]
    for i in range(a):
        for j in range(0, cols, tile):
            l = jnp.dot(xs, w_ref[i, :, j : j + tile], preferred_element_type=jnp.float32)
            at = i * cols + j
            logit[:, at : at + tile] = l
            for n in range(0, tile, 128):
                piece = l[:, n : n + 128]
                part = piece if part is None else jnp.maximum(part, piece)
            low = l.astype(jnp.bfloat16)
            ids = lax.broadcasted_iota(jnp.int32, (tile, slots), 0) + (base_ref[0] + at)
            for q in range(recs):
                hot = (ids == lab_ref[q]).astype(jnp.float32).astype(jnp.bfloat16)
                got = jnp.dot(low[q * frames : (q + 1) * frames], hot, preferred_element_type=jnp.float32)
                acc[q] = got if acc[q] is None else acc[q] + got
    top = jnp.max(part, 1, keepdims=True)
    total = jnp.zeros((rows, 128), jnp.float32)
    for n in range(0, a * cols, 128):
        total = total + jnp.exp(logit[:, n : n + 128] - top)
    total = jnp.sum(total, 1, keepdims=True)
    lane = lax.broadcasted_iota(jnp.int32, (frames, 128), 1)
    for q in range(recs):
        pick_ref[q] = acc[q].astype(jnp.bfloat16)
        part_rows = slice(q * frames, (q + 1) * frames)
        both = jnp.where(lane == 0, top[part_rows], total[part_rows])
        stat_ref[q] = both.T[:8]


def exchange_kernel(a, b, V, pick, stat, po, so, pin, sin, pout, sout, sp1, rp1, ss1, rs1, sp, rp, ss, rs):
    r = lax.axis_index("rec")
    v = lax.axis_index("vocab")
    m, k = r // a, r % a
    half = V // 2
    side = v % 2
    me = m * half + v // 2
    n = b * half
    sibling = (r, flip(v, 1))
    peer = lambda d: (((me + d) % n) // half * a + k, ((me + d) % n) % half * 2 + side)
    barrier = pltpu.get_barrier_semaphore()
    for to in [sibling] + [peer(d) for d in range(1, n)]:
        pl.semaphore_signal(barrier, inc=1, device_id=to, device_id_type=MESH)
    pl.semaphore_wait(barrier, n)

    def remote(src, dst, s, t, to):
        return pltpu.make_async_remote_copy(
            src_ref=src, dst_ref=dst, send_sem=s, recv_sem=t, device_id=to, device_id_type=MESH
        )

    copies = []
    for e in range(n):
        copies.append(remote(pick.at[e, 1 - side], pin.at[e], sp1.at[e], rp1.at[e], sibling))
        copies.append(remote(stat.at[e, 1 - side], sin.at[e], ss1.at[e], rs1.at[e], sibling))
    for c in copies:
        c.start()
    row = lax.broadcasted_iota(jnp.int32, sin.shape[1:], 1)
    for e in range(n):
        copies[2 * e].wait_recv()
        copies[2 * e + 1].wait_recv()
        pout[e] = pick[e, side] + pin[e]
        mine, other = stat[e, side], sin[e]
        top = jnp.maximum(mine[:, 0:1], other[:, 0:1])
        total = mine * jnp.exp(mine[:, 0:1] - top) + other * jnp.exp(other[:, 0:1] - top)
        sout[e] = jnp.where(row == 0, top, total)
    for d in range(1, n):
        to = (me + d) % n
        for src, dst, s, t in ((pout, po, sp, rp), (sout, so, ss, rs)):
            c = remote(src.at[to], dst.at[me], s.at[d - 1], t.at[d - 1], peer(d))
            c.start()
            copies.append(c)
    po[me] = pout[me]
    so[me] = sout[me]
    for d in range(1, n):
        fr = (me + n - d) % n
        for src, dst, s, t in ((pout, po, sp, rp), (sout, so, ss, rs)):
            remote(src.at[fr], dst.at[fr], s.at[d - 1], t.at[d - 1], peer(d)).wait_recv()
    for c in copies:
        c.wait_send()


def align_kernel(alen, tlen, pick, stat, lp_ref, out_ref):
    n, own, frames, slots = pick.shape
    lane = lax.broadcasted_iota(jnp.int32, (1, slots), 1)
    for q in range(own):
        top = stat[0, q, 0:1, :]
        for i in range(1, n):
            top = jnp.maximum(top, stat[i, q, 0:1, :])
        total = jnp.zeros_like(top)
        for i in range(n):
            total = total + stat[i, q, 1:2, :] * jnp.exp(stat[i, q, 0:1, :] - top)
        norm = top + jnp.log(total)
        got = pick[0, q].astype(jnp.float32)
        for i in range(1, n):
            got = got + pick[i, q].astype(jnp.float32)
        lp_ref[q] = got - jnp.broadcast_to(norm, (slots, frames)).T
        last = alen[q] - 1
        first = jnp.where(lane == 0, lp_ref[q, 0:1, :], NEG)

        def block(t, steps, cur, best):
            emit = [lp_ref[q, pl.ds(t + i, 1), :] for i in range(steps)]
            rolled = [[e if c == 0 else pltpu.roll(e, c, 1) for c in range(steps - i)] for i, e in enumerate(emit)]
            moved = [cur] + [jnp.where(lane < c, NEG, pltpu.roll(cur, c, 1)) for c in range(1, steps + 1)]
            for i in range(steps):
                moved = [jnp.maximum(moved[c], moved[c + 1]) + rolled[i][c] for c in range(steps - i)]
                best = jnp.where(last == t + i, moved[0], best)
            return moved[0], best

        whole = (frames - 1) // run
        cur, best = lax.fori_loop(0, whole, lambda i, c: block(1 + i * run, run, *c), (first, first))
        if (frames - 1) % run:
            best = block(1 + whole * run, (frames - 1) % run, cur, best)[1]
        score = jnp.sum(jnp.where(lane == tlen[q] - 1, best, 0.0), 1, keepdims=True)
        out_ref[q] = jnp.broadcast_to(score, (8, 128))


def body(features, head_weight, labels, audio_len, transcript_len):
    rec_dev, frames, width = features.shape
    cols = head_weight.shape[1]
    slots = labels.shape[1]
    G, V = lax.axis_size("rec"), lax.axis_size("vocab")
    best = None
    a = 2
    while a < G:
        cost = (a - 1) * width * cols + (G // a - 1) * features.size
        if G % a == 0 and (best is None or cost < best[0]):
            best = (cost, a)
        a *= 2
    a = best[1]
    b = G // a
    own = rec_dev // V
    vmem = pl.BlockSpec(memory_space=pltpu.VMEM)
    hbm = pl.BlockSpec(memory_space=pl.ANY)
    smem = pl.BlockSpec(memory_space=pltpu.SMEM)
    dma = pltpu.SemaphoreType.DMA
    xg, wg, lg = pl.pallas_call(
        functools.partial(gather_kernel, a, b, V),
        out_shape=(
            jax.ShapeDtypeStruct((b,) + features.shape, features.dtype),
            jax.ShapeDtypeStruct((a,) + head_weight.shape, head_weight.dtype),
            jax.ShapeDtypeStruct((b, rec_dev, 1, slots), jnp.int32),
        ),
        in_specs=[vmem] * 3,
        out_specs=(hbm, hbm, hbm),
        scratch_shapes=[
            dma((a - 1,)), dma((a - 1,)), dma((b - 1,)), dma((b - 1,)),
            dma((b - 1,)), dma((b - 1, V)), dma(((b - 1) * (V - 1),)), dma((3,)),
        ],
        compiler_params=pltpu.CompilerParams(collective_id=0, has_side_effects=True),
        name="gather",
    )(features, head_weight, labels.reshape(rec_dev, 1, slots))

    r, v = lax.axis_index("rec"), lax.axis_index("vocab")
    base = ((v * G + (r // a) * a) * cols).astype(jnp.int32).reshape(1)
    total = b * rec_dev
    recs = 2 if total % 2 == 0 else 1
    tile = min(512, cols)
    pick, stat = pl.pallas_call(
        functools.partial(score_kernel, recs, tile),
        grid=(total // recs,),
        out_shape=(
            jax.ShapeDtypeStruct((total, frames, slots), jnp.bfloat16),
            jax.ShapeDtypeStruct((total, 8, frames), jnp.float32),
        ),
        in_specs=[
            smem,
            pl.BlockSpec((recs, frames, width), lambda i: (i, 0, 0)),
            pl.BlockSpec((a, width, cols), lambda i: (0, 0, 0)),
            pl.BlockSpec((recs, 1, slots), lambda i: (i, 0, 0)),
        ],
        out_specs=(
            pl.BlockSpec((recs, frames, slots), lambda i: (i, 0, 0)),
            pl.BlockSpec((recs, 8, frames), lambda i: (i, 0, 0)),
        ),
        scratch_shapes=[pltpu.VMEM((recs * frames, a * cols), jnp.float32)],
        compiler_params=pltpu.CompilerParams(vmem_limit_bytes=60 * 1024 * 1024),
        name="score",
    )(base, xg.reshape(total, frames, width), wg, lg.reshape(total, 1, slots))

    n = b * (V // 2)
    pick = pick.reshape(n, 2, own, frames, slots)
    stat = stat.reshape(n, 2, own, 8, frames)
    picked = (n, own, frames, slots)
    stats = (n, own, 8, frames)
    po, so = pl.pallas_call(
        functools.partial(exchange_kernel, a, b, V),
        out_shape=(
            jax.ShapeDtypeStruct(picked, pick.dtype),
            jax.ShapeDtypeStruct(stats, stat.dtype),
        ),
        in_specs=[vmem] * 2,
        out_specs=(vmem, vmem),
        scratch_shapes=[pltpu.VMEM(picked, pick.dtype), pltpu.VMEM(stats, stat.dtype)] * 2
        + [dma((n,))] * 4
        + [dma((n - 1,))] * 4,
        compiler_params=pltpu.CompilerParams(collective_id=1, has_side_effects=True),
        name="exchange",
    )(pick, stat)

    log_prob, score = pl.pallas_call(
        align_kernel,
        out_shape=(
            jax.ShapeDtypeStruct((own, frames, slots), jnp.float32),
            jax.ShapeDtypeStruct((own, 8, 128), jnp.float32),
        ),
        in_specs=[smem, smem, vmem, vmem],
        out_specs=(vmem, vmem),
        name="align",
    )(audio_len, transcript_len, po, so)
    return log_prob, score[:, 0, 0]


def solution(mesh):
    return jax.shard_map(
        body,
        mesh=mesh,
        in_specs=(
            P("rec", None, None),
            P(None, ("vocab", "rec")),
            P("rec", None),
            P(("rec", "vocab")),
            P(("rec", "vocab")),
        ),
        out_specs=(P(("rec", "vocab"), None, None), P(("rec", "vocab"))),
        check_vma=False,
    )
```

profile of v0, /device:TPU:0, one launch (start us, length us, event | category | flops | bytes accessed | tf_op | source)
XLA Modules:
  0.0 128.0 jit_solution(12115947750742424933)
XLA Ops:
  0.6 66.0 %gather.1 = (bf16[4,4,192,1280]{3,2,1,0:T(8,128)(2,1)}, bf16[2,1280,1024]{2,1,0:T(8,128)(2,1)}, s32[4,4,1,128]{3,2,1,0:T(1,128)}) custom-call(bf16[4,192,1280]{2,1,0:T(8,128)(2,1)} %x.1, bf16[1280,1024]{1,0:T(8,128)(2,1)} %w.1, s32[4,1,128]{2,1,0:T(1,128)} %bitcast.11), custom_call_target="tpu_custom_call" | custom-call | tf_op jit(solution)/shard_map/gather/pallas_call | solution.py:237
  66.6 29.2 %score.1 = (bf16[16,192,128]{2,1,0:T(8,128)(2,1)}, f32[16,8,192]{2,1,0:T(8,128)}) custom-call(s32[1]{0:T(128)} %bitcast.base_ref, bf16[16,192,1280]{2,1,0:T(8,128)(2,1)} %bitcast.7, bf16[2,1280,1024]{2,1,0:T(8,128)(2,1)} %get-tuple-element.12.w_ref, s32[16,1,128]{2,1,0:T(1,128)} %bitcast.10), custom_call_target="tpu_custom_call" | custom-call | tf_op jit(solution)/shard_map/score/pallas_call | solution.py:259
  95.8 24.8 %exchange.1 = (bf16[8,1,192,128]{3,2,1,0:T(8,128)(2,1)}, f32[8,1,8,192]{3,2,1,0:T(8,128)}) custom-call(bf16[8,2,1,192,128]{4,3,2,1,0:T(8,128)(2,1)} %bitcast.8, f32[8,2,1,8,192]{4,3,2,1,0:T(8,128)} %bitcast.9), custom_call_target="tpu_custom_call" | custom-call | tf_op jit(solution)/shard_map/exchange/pallas_call | solution.py:286
  122.0 4.8 %align.1 = (f32[1,192,128]{2,1,0:T(8,128)}, f32[1,8,128]{2,1,0:T(8,128)}) custom-call(s32[1]{0:T(128)S(6)} %copy.7.alen, s32[1]{0:T(128)S(6)} %copy.8.tlen, bf16[8,1,192,128]{3,2,1,0:T(8,128)(2,1)} %get-tuple-element.16.pick, f32[8,1,8,192]{3,2,1,0:T(8,128)} %get-tuple-element.17.stat), custom_call_target="tpu_custom_call" | custom-call | tf_op jit(solution)/shard_map/align/pallas_call | solution.py:301
  126.8 1.2 slice.3
where the time goes:
time: 129 us; the launch traced here: 128 us
  Pallas kernels  125 us (97%)
  between operations  1.96 us (2%)
    pallas_call x1, Pallas kernels, body(): pl.pallas_call(functools.partial(gather_kernel, a, b, V), out_shape=(jax....  66 us
    pallas_call x1, Pallas kernels, body(): pl.pallas_call(functools.partial(score_kernel, recs, tile), grid=(total /...  29.2 us
    pallas_call x1, Pallas kernels, body(): pl.pallas_call(functools.partial(exchange_kernel, a, b, V), out_shape=(ja...  24.8 us
    pallas_call x1, Pallas kernels, body(): pl.pallas_call(align_kernel, out_shape=(jax.ShapeDtypeStruct((own, frames...  4.8 us

commit v1 on v0

v1 whole, which is shorter than its diff:
```python
import functools
import jax
import jax.numpy as jnp
from jax import lax
from jax.experimental import pallas as pl
from jax.experimental.pallas import tpu as pltpu
from jax.sharding import PartitionSpec as P

MESH = pl.DeviceIdType.MESH
NEG = -1e30
LOW = -3e38
run = 6


def bits_of(size):
    bits = []
    bit = size // 2
    while bit >= 1:
        bits.append(bit)
        bit //= 2
    return bits


def flip(v, mask, size):
    for bit in bits_of(size):
        if mask & bit:
            v = v + bit * (1 - 2 * ((v // bit) % 2))
    return v


def emit_kernel(a, b, V, x, w, lab, pick, stat, xg, wg, lg, mx, sm, acc, sw, rw, sl, rl, sf, rf, sg, loc):
    r = lax.axis_index("rec")
    v = lax.axis_index("vocab")
    G = a * b
    m, k = r // a, r % a
    rec_dev, frames, width = x.shape
    own = rec_dev // V
    nc, cw = wg.shape[1], wg.shape[3]
    cols = nc * cw
    slots = lab.shape[2]
    half = V // 2
    bits = bits_of(V)
    col_peer = lambda d: (m * a + flip(k, d, a), v)
    row_peer = lambda d: (flip(m, d, b) * a + k, v)

    local = [pltpu.make_async_copy(x, xg.at[m], loc.at[0]), pltpu.make_async_copy(lab, lg.at[m], loc.at[1])]
    for c in range(nc):
        local.append(pltpu.make_async_copy(w.at[:, pl.ds(c * cw, cw)], wg.at[k, c], loc.at[2 + c]))
    for c in local:
        c.start()

    barrier = pltpu.get_barrier_semaphore()
    peers = [col_peer(d) for d in range(1, a)] + [row_peer(d) for d in range(1, b)]
    peers += [(r, flip(v, bit, V)) for bit in bits]
    for peer in peers:
        pl.semaphore_signal(barrier, inc=1, device_id=peer, device_id_type=MESH)
    pl.semaphore_wait(barrier, len(peers))
    for c in local:
        c.wait()

    def remote(ref, ss, rs, to):
        return pltpu.make_async_remote_copy(
            src_ref=ref, dst_ref=ref, send_sem=ss, recv_sem=rs, device_id=to, device_id_type=MESH
        )

    sent = []

    def launch(*args):
        c = remote(*args)
        c.start()
        sent.append(c)

    piece = lambda g, c: xg.at[g, pl.ds(c * own, own)]
    for d in range(1, b):
        launch(lg.at[m], sl.at[d - 1], rl.at[d - 1], row_peer(d))
    for c in range(nc):
        for d in range(1, a):
            launch(wg.at[k, c], sw.at[d - 1, c], rw.at[d - 1, c], col_peer(d))
    for d in range(1, b):
        launch(piece(m, v), sf.at[d - 1], rf.at[d - 1, 0], row_peer(d))

    used = [0]

    def arrive_piece(d, mask):
        low = (mask & -mask) if mask else V
        g = flip(m, d, b)
        src = piece(g, flip(v, mask, V))
        remote(src, sf.at[d - 1], rf.at[d - 1, mask], row_peer(d)).wait_recv()
        for bit in bits:
            if bit < low:
                launch(src, sg.at[used[0]], rf.at[d - 1, mask | bit], (r, flip(v, bit, V)))
                used[0] += 1

    def arrive_pair(p):
        d, h = order[p]
        if d == 0:
            return
        if h == 0:
            remote(lg.at[flip(m, d, b)], sl.at[d - 1], rl.at[d - 1], row_peer(d)).wait_recv()
        arrive_piece(d, 2 * h)
        arrive_piece(d, 2 * h + 1)

    def arrive_chunk(e):
        d, c = e // nc, e % nc
        if d:
            ref = wg.at[flip(k, d, a), c]
            remote(ref, sw.at[d - 1, c], rw.at[d - 1, c], col_peer(d)).wait_recv()

    unit = 2 * own
    rows = unit * frames
    order = [(d, h) for d in range(b) for h in range(half)]

    def place(d, h):
        return jnp.bitwise_xor(m, d), jnp.bitwise_xor(v // 2, h)

    def task(p, d, h, e):
        g, pr = place(d, h)
        ke = jnp.bitwise_xor(k, e // nc)
        c = e % nc
        xs = xg[g, pl.ds(pr * unit, unit)].reshape(rows, width)
        l = jnp.dot(xs, wg[ke, c], preferred_element_type=jnp.float32)
        old = mx[p]
        new = old
        for n in range(0, cw, 128):
            new = jnp.maximum(new, l[:, n : n + 128])
        s = sm[p] * jnp.exp(old - new)
        for n in range(0, cw, 128):
            s = s + jnp.exp(l[:, n : n + 128] - new)
        mx[p] = new
        sm[p] = s
        low = l.astype(jnp.bfloat16)
        base = (v * G + m * a + ke) * cols + c * cw
        ids = lax.broadcasted_iota(jnp.int32, (cw, slots), 0) + base
        for q in range(unit):
            hot = (ids == lg[g, pr * unit + q]).astype(jnp.float32).astype(jnp.bfloat16)
            got = jnp.dot(low[q * frames : (q + 1) * frames], hot, preferred_element_type=jnp.float32)
            acc[p, q] = acc[p, q] + got

    def clear(p, _):
        mx[p] = jnp.full((rows, 128), LOW, jnp.float32)
        sm[p] = jnp.zeros((rows, 128), jnp.float32)
        acc[p] = jnp.zeros((unit, frames, slots), jnp.float32)
        return 0

    pairs = b * half
    chunks = a * nc
    lax.fori_loop(0, pairs, clear, 0)

    when = []
    for p, (d, h) in enumerate(order):
        when.append((0.0 if d == 0 else 0.20 + 0.28 * (d - 1) + 0.18 * h, 0, p))
    for e in range(nc, chunks):
        when.append(((e - nc + 1) / nc, 1, e))
    when.sort()
    have_p, have_e = 0, nc

    for _, kind, i in when:
        if kind == 0:
            arrive_pair(i)
            d, h = order[i]
            lax.fori_loop(0, have_e, lambda e, _: (task(i, d, h, e), 0)[1], 0)
            have_p = i + 1
        else:
            arrive_chunk(i)
            lax.fori_loop(0, have_p, lambda p, _: (task(p, p // half, p % half, i), 0)[1], 0)
            have_e = i + 1

    lane = lax.broadcasted_iota(jnp.int32, (frames, 128), 1)

    def finish(p, _):
        g, pr = place(p // half, p % half)
        best = mx[p]
        top = jnp.max(best, 1, keepdims=True)
        total = jnp.sum(sm[p] * jnp.exp(best - top), 1, keepdims=True)
        for q in range(unit):
            at = g * rec_dev + pr * unit + q
            pick[at] = acc[p, q].astype(jnp.bfloat16)
            part = slice(q * frames, (q + 1) * frames)
            stat[at] = jnp.where(lane == 0, top[part], total[part]).T[:8]
        return 0

    lax.fori_loop(0, pairs, finish, 0)
    for c in sent:
        c.wait_send()


def exchange_kernel(a, b, V, pick, stat, po, so, pin, sin, pout, sout, sp1, rp1, ss1, rs1, sp, rp, ss, rs):
    r = lax.axis_index("rec")
    v = lax.axis_index("vocab")
    m, k = r // a, r % a
    half = V // 2
    side = v % 2
    me = m * half + v // 2
    n = b * half
    sibling = (r, flip(v, 1, V))
    peer = lambda d: (((me + d) % n) // half * a + k, ((me + d) % n) % half * 2 + side)
    barrier = pltpu.get_barrier_semaphore()
    for to in [sibling] + [peer(d) for d in range(1, n)]:
        pl.semaphore_signal(barrier, inc=1, device_id=to, device_id_type=MESH)
    pl.semaphore_wait(barrier, n)

    def remote(src, dst, s, t, to):
        return pltpu.make_async_remote_copy(
            src_ref=src, dst_ref=dst, send_sem=s, recv_sem=t, device_id=to, device_id_type=MESH
        )

    copies = []
    for e in range(n):
        copies.append(remote(pick.at[e, 1 - side], pin.at[e], sp1.at[e], rp1.at[e], sibling))
        copies.append(remote(stat.at[e, 1 - side], sin.at[e], ss1.at[e], rs1.at[e], sibling))
    for c in copies:
        c.start()
    row = lax.broadcasted_iota(jnp.int32, sin.shape[1:], 1)
    for e in range(n):
        copies[2 * e].wait_recv()
        copies[2 * e + 1].wait_recv()
        pout[e] = pick[e, side] + pin[e]
        mine, other = stat[e, side], sin[e]
        top = jnp.maximum(mine[:, 0:1], other[:, 0:1])
        total = mine * jnp.exp(mine[:, 0:1] - top) + other * jnp.exp(other[:, 0:1] - top)
        sout[e] = jnp.where(row == 0, top, total)
    for d in range(1, n):
        to = (me + d) % n
        for src, dst, s, t in ((pout, po, sp, rp), (sout, so, ss, rs)):
            c = remote(src.at[to], dst.at[me], s.at[d - 1], t.at[d - 1], peer(d))
            c.start()
            copies.append(c)
    po[me] = pout[me]
    so[me] = sout[me]
    for d in range(1, n):
        fr = (me + n - d) % n
        for src, dst, s, t in ((pout, po, sp, rp), (sout, so, ss, rs)):
            remote(src.at[fr], dst.at[fr], s.at[d - 1], t.at[d - 1], peer(d)).wait_recv()
    for c in copies:
        c.wait_send()


def align_kernel(alen, tlen, pick, stat, lp_ref, out_ref):
    n, own, frames, slots = pick.shape
    lane = lax.broadcasted_iota(jnp.int32, (1, slots), 1)
    for q in range(own):
        top = stat[0, q, 0:1, :]
        for i in range(1, n):
            top = jnp.maximum(top, stat[i, q, 0:1, :])
        total = jnp.zeros_like(top)
        for i in range(n):
            total = total + stat[i, q, 1:2, :] * jnp.exp(stat[i, q, 0:1, :] - top)
        norm = top + jnp.log(total)
        got = pick[0, q].astype(jnp.float32)
        for i in range(1, n):
            got = got + pick[i, q].astype(jnp.float32)
        lp_ref[q] = got - jnp.broadcast_to(norm, (slots, frames)).T
        last = alen[q] - 1
        first = jnp.where(lane == 0, lp_ref[q, 0:1, :], NEG)

        def block(t, steps, cur, best):
            emit = [lp_ref[q, pl.ds(t + i, 1), :] for i in range(steps)]
            rolled = [[e if c == 0 else pltpu.roll(e, c, 1) for c in range(steps - i)] for i, e in enumerate(emit)]
            moved = [cur] + [jnp.where(lane < c, NEG, pltpu.roll(cur, c, 1)) for c in range(1, steps + 1)]
            for i in range(steps):
                moved = [jnp.maximum(moved[c], moved[c + 1]) + rolled[i][c] for c in range(steps - i)]
                best = jnp.where(last == t + i, moved[0], best)
            return moved[0], best

        whole = (frames - 1) // run
        cur, best = lax.fori_loop(0, whole, lambda i, c: block(1 + i * run, run, *c), (first, first))
        if (frames - 1) % run:
            best = block(1 + whole * run, (frames - 1) % run, cur, best)[1]
        score = jnp.sum(jnp.where(lane == tlen[q] - 1, best, 0.0), 1, keepdims=True)
        out_ref[q] = jnp.broadcast_to(score, (8, 128))


def body(features, head_weight, labels, audio_len, transcript_len):
    rec_dev, frames, width = features.shape
    cols = head_weight.shape[1]
    slots = labels.shape[1]
    G, V = lax.axis_size("rec"), lax.axis_size("vocab")
    best = None
    a = 2
    while a < G:
        cost = (a - 1) * width * cols + (G // a - 1) * features.size
        if G % a == 0 and (best is None or cost < best[0]):
            best = (cost, a)
        a *= 2
    a = best[1]
    b = G // a
    own = rec_dev // V
    vmem = pl.BlockSpec(memory_space=pltpu.VMEM)
    hbm = pl.BlockSpec(memory_space=pl.ANY)
    smem = pl.BlockSpec(memory_space=pltpu.SMEM)
    dma = pltpu.SemaphoreType.DMA
    cw = min(256, cols)
    nc = cols // cw
    total = b * rec_dev
    unit = 2 * own
    pairs = b * (V // 2)
    rows = unit * frames
    pick, stat = pl.pallas_call(
        functools.partial(emit_kernel, a, b, V),
        out_shape=(
            jax.ShapeDtypeStruct((total, frames, slots), jnp.bfloat16),
            jax.ShapeDtypeStruct((total, 8, frames), jnp.float32),
        ),
        in_specs=[hbm] * 3,
        out_specs=(vmem, vmem),
        scratch_shapes=[
            pltpu.VMEM((b,) + features.shape, features.dtype),
            pltpu.VMEM((a, nc, width, cw), head_weight.dtype),
            pltpu.VMEM((b, rec_dev, 1, slots), jnp.int32),
            pltpu.VMEM((pairs, rows, 128), jnp.float32),
            pltpu.VMEM((pairs, rows, 128), jnp.float32),
            pltpu.VMEM((pairs, unit, frames, slots), jnp.float32),
            dma((a - 1, nc)), dma((a - 1, nc)), dma((b - 1,)), dma((b - 1,)),
            dma((b - 1,)), dma((b - 1, V)), dma(((b - 1) * (V - 1),)), dma((2 + nc,)),
        ],
        compiler_params=pltpu.CompilerParams(
            collective_id=0, has_side_effects=True, vmem_limit_bytes=60 * 1024 * 1024
        ),
        name="emit",
    )(features, head_weight, labels.reshape(rec_dev, 1, slots))

    n = b * (V // 2)
    pick = pick.reshape(n, 2, own, frames, slots)
    stat = stat.reshape(n, 2, own, 8, frames)
    picked = (n, own, frames, slots)
    stats = (n, own, 8, frames)
    po, so = pl.pallas_call(
        functools.partial(exchange_kernel, a, b, V),
        out_shape=(
            jax.ShapeDtypeStruct(picked, pick.dtype),
            jax.ShapeDtypeStruct(stats, stat.dtype),
        ),
        in_specs=[vmem] * 2,
        out_specs=(vmem, vmem),
        scratch_shapes=[pltpu.VMEM(picked, pick.dtype), pltpu.VMEM(stats, stat.dtype)] * 2
        + [dma((n,))] * 4
        + [dma((n - 1,))] * 4,
        compiler_params=pltpu.CompilerParams(collective_id=1, has_side_effects=True),
        name="exchange",
    )(pick, stat)

    log_prob, score = pl.pallas_call(
        align_kernel,
        out_shape=(
            jax.ShapeDtypeStruct((own, frames, slots), jnp.float32),
            jax.ShapeDtypeStruct((own, 8, 128), jnp.float32),
        ),
        in_specs=[smem, smem, vmem, vmem],
        out_specs=(vmem, vmem),
        name="align",
    )(audio_len, transcript_len, po, so)
    return log_prob, score[:, 0, 0]


def solution(mesh):
    return jax.shard_map(
        body,
        mesh=mesh,
        in_specs=(
            P("rec", None, None),
            P(None, ("vocab", "rec")),
            P("rec", None),
            P(("rec", "vocab")),
            P(("rec", "vocab")),
        ),
        out_specs=(P(("rec", "vocab"), None, None), P(("rec", "vocab"))),
        check_vma=False,
    )
```

time: 129 us -> 115 us (0.89)
  Pallas kernels: 125 us -> 112 us
    pallas_call x2 -> x1, Pallas kernels: 95.2 us -> 88.3 us  [body(): pl.pallas_call(functools.partial(emit_kernel, a, b, V), out_shape=(jax.Sh...]
    pallas_call x1, Pallas kernels: 24.8 us -> 18.4 us  [body(): pl.pallas_call(functools.partial(exchange_kernel, a, b, V), out_shape=(ja...]
where the time goes in v1:
time: 115 us
  Pallas kernels  112 us (97%)
  between operations  1.94 us (2%)
  local copies, waits for them, and re-layouts  1.19 us (1%)
    pallas_call x1, Pallas kernels, body(): pl.pallas_call(functools.partial(emit_kernel, a, b, V), out_shape=(jax.Sh...  88.3 us
    pallas_call x1, Pallas kernels, body(): pl.pallas_call(functools.partial(exchange_kernel, a, b, V), out_shape=(ja...  18.4 us
    pallas_call x1, Pallas kernels, body(): pl.pallas_call(align_kernel, out_shape=(jax.ShapeDtypeStruct((own, frames...  4.79 us

profile of v1, /device:TPU:0, one launch (start us, length us, event | category | flops | bytes accessed | tf_op | source)
XLA Modules:
  0.0 114.6 jit_solution(13807862029440432140)
XLA Ops:
  0.6 88.3 %emit.1 = (bf16[16,192,128]{2,1,0:T(8,128)(2,1)}, f32[16,8,192]{2,1,0:T(8,128)}) custom-call(bf16[4,192,1280]{2,1,0:T(8,128)(2,1)} %x.1, bf16[1280,1024]{1,0:T(8,128)(2,1)} %w.1, s32[4,1,128]{2,1,0:T(1,128)} %bitcast.6), custom_call_target="tpu_custom_call" | custom-call | tf_op jit(solution)/shard_map/emit/pallas_call | solution.py:298
  89.0 18.4 %exchange.1 = (bf16[8,1,192,128]{3,2,1,0:T(8,128)(2,1)}, f32[8,1,8,192]{3,2,1,0:T(8,128)}) custom-call(bf16[8,2,1,192,128]{4,3,2,1,0:T(8,128)(2,1)} %bitcast.4, f32[8,2,1,8,192]{4,3,2,1,0:T(8,128)} %bitcast.5), custom_call_target="tpu_custom_call" | custom-call | tf_op jit(solution)/shard_map/exchange/pallas_call | solution.py:327
  108.6 4.8 %align.1 = (f32[1,192,128]{2,1,0:T(8,128)}, f32[1,8,128]{2,1,0:T(8,128)}) custom-call(s32[1]{0:T(128)S(6)} %copy.7.alen, s32[1]{0:T(128)S(6)} %copy.8.tlen, bf16[8,1,192,128]{3,2,1,0:T(8,128)(2,1)} %get-tuple-element.10.pick, f32[8,1,8,192]{3,2,1,0:T(8,128)} %get-tuple-element.11.stat), custom_call_target="tpu_custom_call" | custom-call | tf_op jit(solution)/shard_map/align/pallas_call | solution.py:342
  113.4 1.2 %slice.3 = f32[1,1,1]{2,1,0:T(1,128)} slice(f32[1,8,128]{2,1,0:T(8,128)} %get-tuple-element.13), slice={[0:1], [0:1], [0:1]} | slice | bytes 8 | tf_op jit(solution)/shard_map/slice | solution.py:352

commit v2 on v1

v2 whole, which is shorter than its diff:
```python
import functools
import jax
import jax.numpy as jnp
from jax import lax
from jax.experimental import pallas as pl
from jax.experimental.pallas import tpu as pltpu
from jax.sharding import PartitionSpec as P

MESH = pl.DeviceIdType.MESH
NEG = -1e30
LOW = -3e38
run = 6


def bits_of(size):
    bits = []
    bit = size // 2
    while bit >= 1:
        bits.append(bit)
        bit //= 2
    return bits


def flip(v, mask, size):
    for bit in bits_of(size):
        if mask & bit:
            v = v + bit * (1 - 2 * ((v // bit) % 2))
    return v


def emit_kernel(
    a, b, V, x, w, lab, pick_ref, stat_ref, xg, wg, lg, mx, sm, acc, logit,
    pp, pin, cs, xin, xout, zin, st, sin, cst, xst, zsrc, zst,
    sw, rw, sl, rl, su, sx, rf, sp, rp, ss, rs, sq, rq, sv, rv, sz, rz, sy, ry, loc,
):
    r = lax.axis_index("rec")
    v = lax.axis_index("vocab")
    G = a * b
    m, k = r // a, r % a
    rec_dev, frames, width = x.shape
    own = rec_dev // V
    nc, cw = wg.shape[1], wg.shape[3]
    cols = nc * cw
    slots = lab.shape[2]
    half = V // 2
    side = v % 2
    bits = bits_of(V)
    unit = 2 * own
    rows = unit * frames
    pairs = b * half
    chunks = a * nc

    def among(values, i):
        out = values[0]
        for j in range(1, len(values)):
            out = jnp.where(i == j, values[j], out)
        return out

    near = [sorted(range(b), key=lambda o: (abs(o - i), o)) for i in range(b)]
    turns = [among([near[i][t] ^ i for i in range(b)], m) for t in range(b)]
    turn = lambda t: turns[t] if isinstance(t, int) else among(turns, t)
    inner = (m > 0) & (m < b - 1)

    col_peer = lambda d: (m * a + flip(k, d, a), v)
    row_peer = lambda d: (flip(m, d, b) * a + k, v)
    line = lambda at: (at * a + k, v)
    sibling = (r, flip(v, 1, V))
    across = lambda h: (r, flip(v, 2 * h, V))

    local = [pltpu.make_async_copy(x, xg.at[m], loc.at[0]), pltpu.make_async_copy(lab, lg.at[m], loc.at[1])]
    for c in range(nc):
        local.append(pltpu.make_async_copy(w.at[:, pl.ds(c * cw, cw)], wg.at[k, c], loc.at[2 + c]))
    for c in local:
        c.start()

    barrier = pltpu.get_barrier_semaphore()
    peers = [col_peer(d) for d in range(1, a)] + [row_peer(d) for d in range(1, b)]
    peers += [(r, flip(v, mask, V)) for mask in sorted(set(bits + [2 * h for h in range(1, half)]))]
    for peer in peers:
        pl.semaphore_signal(barrier, inc=1, device_id=peer, device_id_type=MESH)
    pl.semaphore_wait(barrier, len(peers))
    for c in local:
        c.wait()

    def remote(src, dst, s, t, to):
        return pltpu.make_async_remote_copy(
            src_ref=src, dst_ref=dst, send_sem=s, recv_sem=t, device_id=to, device_id_type=MESH
        )

    sent = []

    def launch(*args):
        c = remote(*args)
        c.start()
        sent.append(c)

    piece = lambda g, c: xg.at[g, pl.ds(c * own, own)]
    for c in range(nc):
        for d in range(1, a):
            ref = wg.at[k, c]
            launch(ref, ref, sw.at[d - 1, c], rw.at[d - 1, c], col_peer(d))
    for d in range(1, b):
        launch(lg.at[m], lg.at[m], sl.at[d - 1], rl.at[d - 1], row_peer(d))

    def pass_on(o, up, go):
        src = piece(o, v)
        to = line(m + 1 if up else m - 1)
        c = remote(src, src, su.at[o, 0 if up else 1], rf.at[o, 0], to)
        pl.when(go)(c.start)

    pass_on(m, True, m < b - 1)
    pass_on(m, False, m > 0)

    def recv_line(t):
        o = jnp.bitwise_xor(m, turn(t))
        src = piece(o, v)
        remote(src, src, sx.at[t, 0], rf.at[o, 0], across(0)).wait_recv()
        pass_on(o, True, (o < m) & (m < b - 1))
        pass_on(o, False, (o > m) & (m > 0))
        for bit in bits:
            remote(src, src, sx.at[t, bit], rf.at[o, bit], (r, flip(v, bit, V))).start()

    def recv_side(t, mask):
        o = jnp.bitwise_xor(m, turn(t))
        low = mask & -mask
        src = piece(o, flip(v, mask, V))
        remote(src, src, sx.at[t, mask], rf.at[o, mask], across(0)).wait_recv()
        for bit in bits:
            if bit < low:
                remote(src, src, sx.at[t, mask | bit], rf.at[o, mask | bit], (r, flip(v, bit, V))).start()

    def recv_chunk(e):
        d, c = e // nc, e % nc
        ref = wg.at[flip(k, d, a), c]
        remote(ref, ref, sw.at[d - 1, c], rw.at[d - 1, c], col_peer(d)).wait_recv()

    def task(which, es):
        for j, (d, h) in enumerate(which):
            p = d * half + h
            g, pr = jnp.bitwise_xor(m, d), jnp.bitwise_xor(v // 2, h)
            xs = xg[g, pl.ds(pr * unit, unit)].reshape(rows, width)
            old = mx[p]
            new = old
            base = []
            for i, e in enumerate(es):
                ke = jnp.bitwise_xor(k, e // nc)
                c = e % nc
                l = jnp.dot(xs, wg[ke, c], preferred_element_type=jnp.float32)
                logit[j, :, i * cw : (i + 1) * cw] = l
                for n in range(0, cw, 128):
                    new = jnp.maximum(new, l[:, n : n + 128])
                low = l.astype(jnp.bfloat16)
                base = (v * G + m * a + ke) * cols + c * cw
                ids = lax.broadcasted_iota(jnp.int32, (cw, slots), 0) + base
                for q in range(unit):
                    hot = (ids == lg[g, pr * unit + q]).astype(jnp.float32).astype(jnp.bfloat16)
                    got = jnp.dot(low[q * frames : (q + 1) * frames], hot, preferred_element_type=jnp.float32)
                    acc[p, q] = acc[p, q] + got
            s = sm[p] * jnp.exp(old - new)
            for n in range(0, len(es) * cw, 128):
                s = s + jnp.exp(logit[j, :, n : n + 128] - new)
            mx[p] = new
            sm[p] = s

    def clear(p, _):
        mx[p] = jnp.full((rows, 128), LOW, jnp.float32)
        sm[p] = jnp.zeros((rows, 128), jnp.float32)
        acc[p] = jnp.zeros((unit, frames, slots), jnp.float32)
        return 0

    def chunks_of(d, h, count):
        lax.fori_loop(0, count // 2, lambda i, _: (task([(d, h)], [2 * i, 2 * i + 1]), 0)[1], 0)
        if count % 2:
            task([(d, h)], [count - 1])

    def pairs_of(count, e):
        at = lambda i: (turn(i // half), i % half)
        lax.fori_loop(0, count // 2, lambda i, _: (task([at(2 * i), at(2 * i + 1)], [e]), 0)[1], 0)
        if count % 2:
            task([at(count - 1)], [e])

    lax.fori_loop(0, pairs, clear, 0)

    events = []
    for t in range(1, b):
        events.append((0.2 * max(t - 1, 1), 0, t, 0))
        events.append((0.2 * t, 1, t, 0))
        for h in range(half):
            events.append((0.2 * t + 0.03 + 0.17 * h, 2, t, h))
    for e in range(nc, chunks - 1):
        events.append(((e - nc + 1) / (chunks - nc), 3, e, 0))
    events.sort()

    lax.fori_loop(0, half, lambda h, _: (chunks_of(0, h, nc), 0)[1], 0)
    have_p, have_e = half, nc
    for _, kind, i, h in events:
        if kind == 0:
            pl.when(inner)(functools.partial(recv_line, i))
        elif kind == 1:
            pl.when(jnp.logical_not(inner))(functools.partial(recv_line, i))
        elif kind == 2:
            if h == 0:
                d = turn(i)
                o = jnp.bitwise_xor(m, d)
                remote(lg.at[o], lg.at[o], sl.at[0], rl.at[d - 1], row_peer(1)).wait_recv()
            if h > 0:
                recv_side(i, 2 * h)
            recv_side(i, 2 * h + 1)
            chunks_of(turn(i), h, have_e)
            have_p += 1
        else:
            recv_chunk(i)
            pairs_of(have_p, i)
            have_e = i + 1

    lane = lax.broadcasted_iota(jnp.int32, (frames, 128), 1)
    tall = 4 * unit

    def merge(p, q):
        odd = lax.broadcasted_iota(jnp.int32, (tall, frames), 0) % 2 == 1
        pt, qt = pltpu.roll(p, 1, 0), pltpu.roll(q, 1, 0)
        top = jnp.maximum(pt, qt)
        total = p * jnp.exp(pt - top) + q * jnp.exp(qt - top)
        return jnp.where(odd, total, jnp.maximum(p, q))

    def finish(n, which):
        tile = jnp.zeros((frames, 128), jnp.float32)
        for j, (d, h) in enumerate(which):
            p = d * half + h
            best = mx[p]
            top = jnp.max(best, 1, keepdims=True)
            total = jnp.sum(sm[p] * jnp.exp(best - top), 1, keepdims=True)
            for q in range(unit):
                part = slice(q * frames, (q + 1) * frames)
                pp[p, q // own, q % own] = acc[p, q].astype(jnp.bfloat16)
                at = 2 * (j * unit + q)
                tile = jnp.where(lane == at, top[part], tile)
                tile = jnp.where(lane == at + 1, total[part], tile)
        st[n] = tile.T[:tall]
        for d, h in which:
            p = d * half + h
            launch(pp.at[p, 1 - side], pin.at[p], sp.at[p], rp.at[p], sibling)
        launch(st.at[n], sin.at[n], ss.at[n], rs.at[n], sibling)

    def join_sibling(n, which):
        for d, h in which:
            p = d * half + h
            remote(pin.at[p], pin.at[p], sp.at[p], rp.at[p], sibling).wait_recv()
            cs[p] = pp[p, side] + pin[p]
            if h:
                launch(cs.at[p], xin.at[d, h - 1], sq.at[p], rq.at[d, h - 1], across(h))
        remote(sin.at[n], sin.at[n], ss.at[n], rs.at[n], sibling).wait_recv()
        cst[n] = merge(st[n], sin[n])
        h = which[0][1]
        if h:
            t = which[0][0] // 2
            launch(cst.at[n], xst.at[t, h - 1], sv.at[n], rv.at[t, h - 1], across(h))

    def join_across(n, which):
        t = which[0][0] // 2
        for d, _ in which:
            total = cs[d * half]
            for h in range(1, half):
                remote(xin.at[d, h - 1], xin.at[d, h - 1], sq.at[0], rq.at[d, h - 1], across(h)).wait_recv()
                total = total + xin[d, h - 1]
            if d:
                xout[d] = total
                launch(xout.at[d], zin.at[d], sz.at[d], rz.at[d], row_peer(d))
            else:
                zin[d] = total
        tile = cst[n]
        for h in range(1, half):
            remote(xst.at[t, h - 1], xst.at[t, h - 1], sv.at[0], rv.at[t, h - 1], across(h)).wait_recv()
            tile = merge(tile, xst[t, h - 1])
        zsrc[t] = tile
        for d, _ in which:
            if d:
                launch(zsrc.at[t], zst.at[d], sy.at[d], ry.at[d], row_peer(d))
            else:
                zst[d] = tile

    recv_chunk(chunks - 1)
    blocks = [[(2 * t + 1, h), (2 * t, h)] for h in reversed(range(half)) for t in reversed(range(b // 2))]
    for n, which in enumerate(blocks):
        task(which, [chunks - 1])
        finish(n, which)
        if n:
            join_sibling(n - 1, blocks[n - 1])
    last = len(blocks) - 1
    join_sibling(last, blocks[last])
    for n, which in enumerate(blocks):
        if which[0][1] == 0:
            join_across(n, which)

    for q in range(own):
        got = zin[0, q]
        for d in range(1, b):
            if q == 0:
                remote(zin.at[d], zin.at[d], sz.at[d], rz.at[d], row_peer(d)).wait_recv()
                remote(zst.at[d], zst.at[d], sy.at[d], ry.at[d], row_peer(d)).wait_recv()
            got = got + zin[d, q]
        pick_ref[q] = got
        tops, sums = [], []
        for d in range(b):
            at = 2 * ((1 - d % 2) * unit + side * own + q)
            tops.append(zst[d, pl.ds(at, 1), :])
            sums.append(zst[d, pl.ds(at + 1, 1), :])
        top = tops[0]
        for one in tops[1:]:
            top = jnp.maximum(top, one)
        total = jnp.zeros_like(top)
        for one, part in zip(tops, sums):
            total = total + part * jnp.exp(one - top)
        stat_ref[q] = jnp.broadcast_to(top + jnp.log(total), (8, frames))

    for c in sent:
        c.wait_send()
    for t in range(1, b):
        o = jnp.bitwise_xor(m, turn(t))
        for mask in range(1, V):
            src = piece(o, v)
            remote(src, src, sx.at[t, mask], rf.at[o, mask], across(0)).wait_send()
    for o in range(b):
        src = piece(o, v)
        pl.when((o <= m) & (m < b - 1))(remote(src, src, su.at[o, 0], rf.at[o, 0], across(0)).wait_send)
        pl.when((o >= m) & (m > 0))(remote(src, src, su.at[o, 1], rf.at[o, 0], across(0)).wait_send)


def align_kernel(alen, tlen, pick, stat, lp_ref, out_ref):
    own, frames, slots = pick.shape
    lane = lax.broadcasted_iota(jnp.int32, (1, slots), 1)
    for q in range(own):
        norm = jnp.broadcast_to(stat[q, 0:1, :], (slots, frames)).T
        lp_ref[q] = pick[q].astype(jnp.float32) - norm
        last = alen[q] - 1
        first = jnp.where(lane == 0, lp_ref[q, 0:1, :], NEG)

        def block(t, steps, cur, best):
            emit = [lp_ref[q, pl.ds(t + i, 1), :] for i in range(steps)]
            rolled = [[e if c == 0 else pltpu.roll(e, c, 1) for c in range(steps - i)] for i, e in enumerate(emit)]
            moved = [cur] + [jnp.where(lane < c, NEG, pltpu.roll(cur, c, 1)) for c in range(1, steps + 1)]
            for i in range(steps):
                moved = [jnp.maximum(moved[c], moved[c + 1]) + rolled[i][c] for c in range(steps - i)]
                best = jnp.where(last == t + i, moved[0], best)
            return moved[0], best

        whole = (frames - 1) // run
        cur, best = lax.fori_loop(0, whole, lambda i, c: block(1 + i * run, run, *c), (first, first))
        if (frames - 1) % run:
            best = block(1 + whole * run, (frames - 1) % run, cur, best)[1]
        score = jnp.sum(jnp.where(lane == tlen[q] - 1, best, 0.0), 1, keepdims=True)
        out_ref[q] = jnp.broadcast_to(score, (8, 128))


def body(features, head_weight, labels, audio_len, transcript_len):
    rec_dev, frames, width = features.shape
    cols = head_weight.shape[1]
    slots = labels.shape[1]
    G, V = lax.axis_size("rec"), lax.axis_size("vocab")
    best = None
    a = 2
    while a < G:
        cost = (a - 1) * width * cols + (G // a - 1) * features.size
        if G % a == 0 and (best is None or cost < best[0]):
            best = (cost, a)
        a *= 2
    a = best[1]
    b = G // a
    own = rec_dev // V
    vmem = pl.BlockSpec(memory_space=pltpu.VMEM)
    hbm = pl.BlockSpec(memory_space=pl.ANY)
    smem = pl.BlockSpec(memory_space=pltpu.SMEM)
    dma = pltpu.SemaphoreType.DMA
    cw = min(256, cols)
    nc = cols // cw
    unit = 2 * own
    pairs = b * (V // 2)
    rows = unit * frames
    bf, f32 = jnp.bfloat16, jnp.float32
    half = V // 2
    tall = 4 * unit
    one = (own, frames, slots)
    pick, stat = pl.pallas_call(
        functools.partial(emit_kernel, a, b, V),
        out_shape=(jax.ShapeDtypeStruct(one, bf), jax.ShapeDtypeStruct((own, 8, frames), f32)),
        in_specs=[hbm] * 3,
        out_specs=(vmem, vmem),
        scratch_shapes=[
            pltpu.VMEM((b,) + features.shape, features.dtype),
            pltpu.VMEM((a, nc, width, cw), head_weight.dtype),
            pltpu.VMEM((b, rec_dev, 1, slots), jnp.int32),
            pltpu.VMEM((pairs, rows, 128), f32),
            pltpu.VMEM((pairs, rows, 128), f32),
            pltpu.VMEM((pairs, unit, frames, slots), f32),
            pltpu.VMEM((2, rows, 2 * cw), f32),
            pltpu.VMEM((pairs, 2) + one, bf),
            pltpu.VMEM((pairs,) + one, bf),
            pltpu.VMEM((pairs,) + one, bf),
            pltpu.VMEM((b, half - 1) + one, bf),
            pltpu.VMEM((b,) + one, bf),
            pltpu.VMEM((b,) + one, bf),
            pltpu.VMEM((pairs // 2, tall, frames), f32),
            pltpu.VMEM((pairs // 2, tall, frames), f32),
            pltpu.VMEM((pairs // 2, tall, frames), f32),
            pltpu.VMEM((b // 2, half - 1, tall, frames), f32),
            pltpu.VMEM((b // 2, tall, frames), f32),
            pltpu.VMEM((b, tall, frames), f32),
            dma((a - 1, nc)), dma((a - 1, nc)), dma((b - 1,)), dma((b - 1,)),
            dma((b, 2)), dma((b, V)), dma((b, V)),
            dma((pairs,)), dma((pairs,)), dma((pairs // 2,)), dma((pairs // 2,)),
            dma((pairs,)), dma((b, half - 1)), dma((pairs // 2,)), dma((b // 2, half - 1)),
            dma((b,)), dma((b,)), dma((b,)), dma((b,)), dma((2 + nc,)),
        ],
        compiler_params=pltpu.CompilerParams(
            collective_id=0, has_side_effects=True, vmem_limit_bytes=60 * 1024 * 1024
        ),
        name="emit",
    )(features, head_weight, labels.reshape(rec_dev, 1, slots))

    log_prob, score = pl.pallas_call(
        align_kernel,
        out_shape=(
            jax.ShapeDtypeStruct((own, frames, slots), jnp.float32),
            jax.ShapeDtypeStruct((own, 8, 128), jnp.float32),
        ),
        in_specs=[smem, smem, vmem, vmem],
        out_specs=(vmem, vmem),
        name="align",
    )(audio_len, transcript_len, pick, stat)
    return log_prob, score[:, 0, 0]


def solution(mesh):
    return jax.shard_map(
        body,
        mesh=mesh,
        in_specs=(
            P("rec", None, None),
            P(None, ("vocab", "rec")),
            P("rec", None),
            P(("rec", "vocab")),
            P(("rec", "vocab")),
        ),
        out_specs=(P(("rec", "vocab"), None, None), P(("rec", "vocab"))),
        check_vma=False,
    )
```

time: 115 us -> 88.3 us (0.77)
  Pallas kernels: 112 us -> 85 us
    pallas_call x1 -> x0, Pallas kernels: 18.4 us -> none  [body(): pl.pallas_call(functools.partial(exchange_kernel, a, b, V), out_shape=(ja...]
    pallas_call x1, Pallas kernels: 88.3 us -> 80.4 us  [body(): pl.pallas_call(functools.partial(emit_kernel, a, b, V), out_shape=(jax.Sh...]
where the time goes in v2:
time: 88.3 us; the launch traced here: 88.1 us
  Pallas kernels  85 us (96%)
  between operations  1.93 us (2%)
  local copies, waits for them, and re-layouts  1.19 us (1%)
    pallas_call x1, Pallas kernels, body(): pl.pallas_call(functools.partial(emit_kernel, a, b, V), out_shape=(jax.Sh...  80.4 us
    pallas_call x1, Pallas kernels, body(): pl.pallas_call(align_kernel, out_shape=(jax.ShapeDtypeStruct((own, frames...  4.57 us

profile of v2, /device:TPU:0, one launch (start us, length us, event | category | flops | bytes accessed | tf_op | source)
XLA Modules:
  0.0 88.1 jit_solution(15294709865338747721)
XLA Ops:
  1.9 80.4 %emit.1 = (bf16[1,192,128]{2,1,0:T(8,128)(2,1)}, f32[1,8,192]{2,1,0:T(8,128)}) custom-call(bf16[4,192,1280]{2,1,0:T(8,128)(2,1)} %x.1, bf16[1280,1024]{1,0:T(8,128)(2,1)} %w.1, s32[4,1,128]{2,1,0:T(1,128)} %bitcast.2), custom_call_target="tpu_custom_call" | custom-call | tf_op jit(solution)/shard_map/emit/pallas_call | solution.py:383
  82.3 4.6 %align.1 = (f32[1,192,128]{2,1,0:T(8,128)}, f32[1,8,128]{2,1,0:T(8,128)}) custom-call(s32[1]{0:T(128)S(6)} %copy.7.alen, s32[1]{0:T(128)S(6)} %copy.8.tlen, bf16[1,192,128]{2,1,0:T(8,128)(2,1)} %get-tuple-element.6.pick, f32[1,8,192]{2,1,0:T(8,128)} %get-tuple-element.7.stat), custom_call_target="tpu_custom_call" | custom-call | tf_op jit(solution)/shard_map/align/pallas_call | solution.py:420
  86.9 1.2 %slice.3 = f32[1,1,1]{2,1,0:T(1,128)} slice(f32[1,8,128]{2,1,0:T(8,128)} %get-tuple-element.9), slice={[0:1], [0:1], [0:1]} | slice | bytes 8 | tf_op jit(solution)/shard_map/slice | solution.py:430

commit v3 on v2

--- a/solution.py
+++ b/solution.py
@@ -9,7 +9,7 @@
 MESH = pl.DeviceIdType.MESH
 NEG = -1e30
 LOW = -3e38
-run = 6
+run = 8
 
 
 def bits_of(size):
@@ -26,6 +26,59 @@
         if mask & bit:
             v = v + bit * (1 - 2 * ((v // bit) % 2))
     return v
+
+
+def best_path(q, last, goal, lp_ref, right, left):
+    own, frames, slots = lp_ref.shape
+    lane = lax.broadcasted_iota(jnp.int32, (1, slots), 1)
+    whole = lp_ref[q]
+    for c in range(1, run):
+        right[c - 1] = pltpu.roll(whole, c, 1)
+    for c in range(1, run + 1):
+        left[c - 1] = pltpu.roll(whole, slots - c, 1)
+    mid = frames // 2
+
+    def row(shifted, c, t):
+        return lp_ref[q, pl.ds(t, 1), :] if c == 0 else shifted[c - 1, pl.ds(t, 1), :]
+
+    def forward(t, steps, cur, best):
+        moved = [cur] + [jnp.where(lane < c, NEG, pltpu.roll(cur, c, 1)) for c in range(1, steps + 1)]
+        for i in range(steps):
+            moved = [jnp.maximum(moved[c], moved[c + 1]) + row(right, c, t + i) for c in range(steps - i)]
+            best = jnp.where(last == t + i, moved[0], best)
+        return moved[0], best
+
+    ends = [jnp.where(lane + c == goal, 0.0, NEG) for c in range(run + 1)]
+
+    def backward(t, steps, cur):
+        moved = [cur] + [jnp.where(lane >= slots - c, NEG, pltpu.roll(cur, slots - c, 1)) for c in range(1, steps + 1)]
+        for i in range(steps):
+            moved = [jnp.where(last == t - i, ends[c], moved[c]) + row(left, c, t - i) for c in range(steps - i + 1)]
+            moved = [jnp.maximum(moved[c], moved[c + 1]) for c in range(steps - i)]
+        return moved[0]
+
+    first = jnp.where(lane == 0, lp_ref[q, 0:1, :], NEG)
+    ahead, behind = mid - 1, frames - mid
+    count = min(ahead, behind) // run
+
+    def both(i, carry):
+        cur, best, tail = carry
+        cur, best = forward(1 + i * run, run, cur, best)
+        return cur, best, backward(frames - 1 - i * run, run, tail)
+
+    cur, best, tail = lax.fori_loop(0, count, both, (first, first, jnp.full((1, slots), NEG, jnp.float32)))
+    done = count * run
+    at = done
+    while at < ahead:
+        cur, best = forward(1 + at, min(run, ahead - at), cur, best)
+        at += min(run, ahead - at)
+    at = done
+    while at < behind:
+        tail = backward(frames - 1 - at, min(run, behind - at), tail)
+        at += min(run, behind - at)
+    early = jnp.sum(jnp.where(lane == goal, best, 0.0), 1, keepdims=True)
+    late = jnp.max(cur + tail, 1, keepdims=True)
+    return jnp.where(last < mid, early, late)
 
 
 def emit_kernel(
@@ -74,13 +127,19 @@
         c.start()
 
     barrier = pltpu.get_barrier_semaphore()
-    peers = [col_peer(d) for d in range(1, a)] + [row_peer(d) for d in range(1, b)]
+    peers = [col_peer(d) for d in range(1, a)]
     peers += [(r, flip(v, mask, V)) for mask in sorted(set(bits + [2 * h for h in range(1, half)]))]
+
+    def greet(peer):
+        pl.semaphore_signal(barrier, inc=1, device_id=peer, device_id_type=MESH)
+
     for peer in peers:
-        pl.semaphore_signal(barrier, inc=1, device_id=peer, device_id_type=MESH)
-    pl.semaphore_wait(barrier, len(peers))
-    for c in local:
-        c.wait()
+        greet(peer)
+    pl.when(m < b - 1)(lambda: greet(line(m + 1)))
+    pl.when(m > 0)(lambda: greet(line(m - 1)))
+    pl.semaphore_wait(barrier, len(peers) + jnp.minimum(m, 1) + jnp.minimum(b - 1 - m, 1))
+    local[0].wait()
+    local[1].wait()
 
     def remote(src, dst, s, t, to):
         return pltpu.make_async_remote_copy(
@@ -98,15 +157,18 @@
     for c in range(nc):
         for d in range(1, a):
             ref = wg.at[k, c]
-            launch(ref, ref, sw.at[d - 1, c], rw.at[d - 1, c], col_peer(d))
-    for d in range(1, b):
-        launch(lg.at[m], lg.at[m], sl.at[d - 1], rl.at[d - 1], row_peer(d))
-
+            launch(w.at[:, pl.ds(c * cw, cw)], ref, sw.at[d - 1, c], rw.at[d - 1, c], col_peer(d))
     def pass_on(o, up, go):
         src = piece(o, v)
         to = line(m + 1 if up else m - 1)
         c = remote(src, src, su.at[o, 0 if up else 1], rf.at[o, 0], to)
-        pl.when(go)(c.start)
+        tags = remote(lg.at[o], lg.at[o], sl.at[o, 0 if up else 1], rl.at[o], to)
+
+        def start():
+            tags.start()
+            c.start()
+
+        pl.when(go)(start)
 
     pass_on(m, True, m < b - 1)
     pass_on(m, False, m > 0)
@@ -114,6 +176,7 @@
     def recv_line(t):
         o = jnp.bitwise_xor(m, turn(t))
         src = piece(o, v)
+        remote(lg.at[o], lg.at[o], sl.at[o, 0], rl.at[o], across(0)).wait_recv()
         remote(src, src, sx.at[t, 0], rf.at[o, 0], across(0)).wait_recv()
         pass_on(o, True, (o < m) & (m < b - 1))
         pass_on(o, False, (o > m) & (m > 0))
@@ -179,6 +242,8 @@
         if count % 2:
             task([at(count - 1)], [e])
 
+    for c in local[2:]:
+        c.wait()
     lax.fori_loop(0, pairs, clear, 0)
 
     events = []
@@ -199,10 +264,6 @@
         elif kind == 1:
             pl.when(jnp.logical_not(inner))(functools.partial(recv_line, i))
         elif kind == 2:
-            if h == 0:
-                d = turn(i)
-                o = jnp.bitwise_xor(m, d)
-                remote(lg.at[o], lg.at[o], sl.at[0], rl.at[d - 1], row_peer(1)).wait_recv()
             if h > 0:
                 recv_side(i, 2 * h)
             recv_side(i, 2 * h + 1)
@@ -279,6 +340,19 @@
             else:
                 zst[d] = tile
 
+    for c in sent[: (a - 1) * (nc - 1)]:
+        c.wait_send()
+    del sent[: (a - 1) * (nc - 1)]
+    for t in range(1, b):
+        o = jnp.bitwise_xor(m, turn(t))
+        for mask in range(1, V):
+            src = piece(o, v)
+            remote(src, src, sx.at[t, mask], rf.at[o, mask], across(0)).wait_send()
+    for o in range(b):
+        src, tag = piece(o, v), lg.at[o]
+        for i, go in enumerate(((o <= m) & (m < b - 1), (o >= m) & (m > 0))):
+            pl.when(go)(remote(src, src, su.at[o, i], rf.at[o, 0], across(0)).wait_send)
+            pl.when(go)(remote(tag, tag, sl.at[o, i], rl.at[o], across(0)).wait_send)
     recv_chunk(chunks - 1)
     blocks = [[(2 * t + 1, h), (2 * t, h)] for h in reversed(range(half)) for t in reversed(range(b // 2))]
     for n, which in enumerate(blocks):
@@ -299,7 +373,6 @@
                 remote(zin.at[d], zin.at[d], sz.at[d], rz.at[d], row_peer(d)).wait_recv()
                 remote(zst.at[d], zst.at[d], sy.at[d], ry.at[d], row_peer(d)).wait_recv()
             got = got + zin[d, q]
-        pick_ref[q] = got
         tops, sums = [], []
         for d in range(b):
             at = 2 * ((1 - d % 2) * unit + side * own + q)
@@ -311,45 +384,23 @@
         total = jnp.zeros_like(top)
         for one, part in zip(tops, sums):
             total = total + part * jnp.exp(one - top)
+        pick_ref[q] = got
         stat_ref[q] = jnp.broadcast_to(top + jnp.log(total), (8, frames))
 
     for c in sent:
         c.wait_send()
-    for t in range(1, b):
-        o = jnp.bitwise_xor(m, turn(t))
-        for mask in range(1, V):
-            src = piece(o, v)
-            remote(src, src, sx.at[t, mask], rf.at[o, mask], across(0)).wait_send()
-    for o in range(b):
-        src = piece(o, v)
-        pl.when((o <= m) & (m < b - 1))(remote(src, src, su.at[o, 0], rf.at[o, 0], across(0)).wait_send)
-        pl.when((o >= m) & (m > 0))(remote(src, src, su.at[o, 1], rf.at[o, 0], across(0)).wait_send)
-
-
-def align_kernel(alen, tlen, pick, stat, lp_ref, out_ref):
+
+
+def align_kernel(alen, tlen, pick, stat, lp_ref, out_ref, right, left):
     own, frames, slots = pick.shape
-    lane = lax.broadcasted_iota(jnp.int32, (1, slots), 1)
+    lane = lax.broadcasted_iota(jnp.int32, (1, own), 1)
+    scores = jnp.zeros((1, own), jnp.float32)
     for q in range(own):
         norm = jnp.broadcast_to(stat[q, 0:1, :], (slots, frames)).T
         lp_ref[q] = pick[q].astype(jnp.float32) - norm
-        last = alen[q] - 1
-        first = jnp.where(lane == 0, lp_ref[q, 0:1, :], NEG)
-
-        def block(t, steps, cur, best):
-            emit = [lp_ref[q, pl.ds(t + i, 1), :] for i in range(steps)]
-            rolled = [[e if c == 0 else pltpu.roll(e, c, 1) for c in range(steps - i)] for i, e in enumerate(emit)]
-            moved = [cur] + [jnp.where(lane < c, NEG, pltpu.roll(cur, c, 1)) for c in range(1, steps + 1)]
-            for i in range(steps):
-                moved = [jnp.maximum(moved[c], moved[c + 1]) + rolled[i][c] for c in range(steps - i)]
-                best = jnp.where(last == t + i, moved[0], best)
-            return moved[0], best
-
-        whole = (frames - 1) // run
-        cur, best = lax.fori_loop(0, whole, lambda i, c: block(1 + i * run, run, *c), (first, first))
-        if (frames - 1) % run:
-            best = block(1 + whole * run, (frames - 1) % run, cur, best)[1]
-        score = jnp.sum(jnp.where(lane == tlen[q] - 1, best, 0.0), 1, keepdims=True)
-        out_ref[q] = jnp.broadcast_to(score, (8, 128))
+        last, goal = alen[0:1, q : q + 1] - 1, tlen[0:1, q : q + 1] - 1
+        scores = jnp.where(lane == q, best_path(q, last, goal, lp_ref, right, left), scores)
+    out_ref[...] = scores
 
 
 def body(features, head_weight, labels, audio_len, transcript_len):
@@ -369,7 +420,6 @@
     own = rec_dev // V
     vmem = pl.BlockSpec(memory_space=pltpu.VMEM)
     hbm = pl.BlockSpec(memory_space=pl.ANY)
-    smem = pl.BlockSpec(memory_space=pltpu.SMEM)
     dma = pltpu.SemaphoreType.DMA
     cw = min(256, cols)
     nc = cols // cw
@@ -405,7 +455,7 @@
             pltpu.VMEM((b // 2, half - 1, tall, frames), f32),
             pltpu.VMEM((b // 2, tall, frames), f32),
             pltpu.VMEM((b, tall, frames), f32),
-            dma((a - 1, nc)), dma((a - 1, nc)), dma((b - 1,)), dma((b - 1,)),
+            dma((a - 1, nc)), dma((a - 1, nc)), dma((b, 2)), dma((b,)),
             dma((b, 2)), dma((b, V)), dma((b, V)),
             dma((pairs,)), dma((pairs,)), dma((pairs // 2,)), dma((pairs // 2,)),
             dma((pairs,)), dma((b, half - 1)), dma((pairs // 2,)), dma((b // 2, half - 1)),
@@ -419,15 +469,13 @@
 
     log_prob, score = pl.pallas_call(
         align_kernel,
-        out_shape=(
-            jax.ShapeDtypeStruct((own, frames, slots), jnp.float32),
-            jax.ShapeDtypeStruct((own, 8, 128), jnp.float32),
-        ),
-        in_specs=[smem, smem, vmem, vmem],
+        out_shape=(jax.ShapeDtypeStruct(one, f32), jax.ShapeDtypeStruct((1, own), f32)),
+        in_specs=[vmem] * 4,
         out_specs=(vmem, vmem),
+        scratch_shapes=[pltpu.VMEM((run - 1, frames, slots), f32), pltpu.VMEM((run, frames, slots), f32)],
         name="align",
-    )(audio_len, transcript_len, pick, stat)
-    return log_prob, score[:, 0, 0]
+    )(audio_len.reshape(1, own), transcript_len.reshape(1, own), pick, stat)
+    return log_prob, score.reshape(own)
 
 
 def solution(mesh):

time: 88.3 us -> 84.9 us (0.961)
  Pallas kernels: 85 us -> 82.8 us
  local copies, waits for them, and re-layouts: 1.19 us -> 0 us
    pallas_call x1, Pallas kernels: 4.57 us -> 3.26 us  [body(): pl.pallas_call(align_kernel, out_shape=(jax.ShapeDtypeStruct(one, f32), j...]
    slice x1 -> x0, local copies, waits for them, and re-layouts: 1.19 us -> none  [body(): return (log_prob, score[:, 0, 0])]
where the time goes in v3:
time: 84.9 us; the launch traced here: 84.7 us
  Pallas kernels  82.8 us (98%)
  between operations  1.93 us (2%)
    pallas_call x1, Pallas kernels, body(): pl.pallas_call(functools.partial(emit_kernel, a, b, V), out_shape=(jax.Sh...  79.5 us
    pallas_call x1, Pallas kernels, body(): pl.pallas_call(align_kernel, out_shape=(jax.ShapeDtypeStruct(one, f32), j...  3.26 us

profile of v3, /device:TPU:0, one launch (start us, length us, event | category | flops | bytes accessed | tf_op | source)
XLA Modules:
  0.0 84.7 jit_solution(7129004857858520471)
XLA Ops:
  1.9 79.5 %emit.1 = (bf16[1,192,128]{2,1,0:T(8,128)(2,1)}, f32[1,8,192]{2,1,0:T(8,128)}) custom-call(bf16[4,192,1280]{2,1,0:T(8,128)(2,1)} %x.1, bf16[1280,1024]{1,0:T(8,128)(2,1)} %w.1, s32[4,1,128]{2,1,0:T(1,128)} %bitcast.6), custom_call_target="tpu_custom_call" | custom-call | tf_op jit(solution)/shard_map/emit/pallas_call | solution.py:433
  81.5 3.3 %align.1 = (f32[1,192,128]{2,1,0:T(8,128)}, f32[1,1]{1,0:T(1,128)}) custom-call(s32[1,1]{1,0:T(1,128)} %bitcast.4.alen, s32[1,1]{1,0:T(1,128)} %bitcast.5.tlen, bf16[1,192,128]{2,1,0:T(8,128)(2,1)} %get-tuple-element.6.pick, f32[1,8,192]{2,1,0:T(8,128)} %get-tuple-element.7.stat), custom_call_target="tpu_custom_call" | custom-call | tf_op jit(solution)/shard_map/align/pallas_call | solution.py:470

commit v4 on v3

--- a/solution.py
+++ b/solution.py
@@ -138,8 +138,6 @@
     pl.when(m < b - 1)(lambda: greet(line(m + 1)))
     pl.when(m > 0)(lambda: greet(line(m - 1)))
     pl.semaphore_wait(barrier, len(peers) + jnp.minimum(m, 1) + jnp.minimum(b - 1 - m, 1))
-    local[0].wait()
-    local[1].wait()
 
     def remote(src, dst, s, t, to):
         return pltpu.make_async_remote_copy(
@@ -170,6 +168,8 @@
 
         pl.when(go)(start)
 
+    local[0].wait()
+    local[1].wait()
     pass_on(m, True, m < b - 1)
     pass_on(m, False, m > 0)
 
@@ -462,7 +462,7 @@
             dma((b,)), dma((b,)), dma((b,)), dma((b,)), dma((2 + nc,)),
         ],
         compiler_params=pltpu.CompilerParams(
-            collective_id=0, has_side_effects=True, vmem_limit_bytes=60 * 1024 * 1024
+            collective_id=0, has_side_effects=True, vmem_limit_bytes=54700 * 1024
         ),
         name="emit",
     )(features, head_weight, labels.reshape(rec_dev, 1, slots))
@@ -473,6 +473,7 @@
         in_specs=[vmem] * 4,
         out_specs=(vmem, vmem),
         scratch_shapes=[pltpu.VMEM((run - 1, frames, slots), f32), pltpu.VMEM((run, frames, slots), f32)],
+        compiler_params=pltpu.CompilerParams(vmem_limit_bytes=8 * 1024 * 1024),
         name="align",
     )(audio_len.reshape(1, own), transcript_len.reshape(1, own), pick, stat)
     return log_prob, score.reshape(own)

time: 84.9 us -> 84.1 us (level)
  Pallas kernels: 82.8 us -> 81.3 us
where the time goes in v4:
time: 84.1 us; the launch traced here: 83.9 us
  Pallas kernels  81.3 us (97%)
  between operations  1.94 us (2%)
    pallas_call x1, Pallas kernels, body(): pl.pallas_call(functools.partial(emit_kernel, a, b, V), out_shape=(jax.Sh...  78.9 us
    pallas_call x1, Pallas kernels, body(): pl.pallas_call(align_kernel, out_shape=(jax.ShapeDtypeStruct(one, f32), j...  2.46 us

profile of v4, /device:TPU:0, one launch (start us, length us, event | category | flops | bytes accessed | tf_op | source)
XLA Modules:
  0.0 83.9 jit_solution(16569747579561246299)
XLA Ops:
  1.9 0.0 copy-start
  1.9 0.7 copy-done
  2.6 78.9 %emit.1 = (bf16[1,192,128]{2,1,0:T(8,128)(2,1)S(1)}, f32[1,8,192]{2,1,0:T(8,128)S(1)}) custom-call(bf16[4,192,1280]{2,1,0:T(8,128)(2,1)} %x.1, bf16[1280,1024]{1,0:T(8,128)(2,1)} %w.1, s32[4,1,128]{2,1,0:T(1,128)S(1)} %bitcast.6), custom_call_target="tpu_custom_call" | custom-call | tf_op jit(solution)/shard_map/emit/pallas_call | solution.py:433
  81.5 2.5 %align.1 = (f32[1,192,128]{2,1,0:T(8,128)}, f32[1,1]{1,0:T(1,128)}) custom-call(s32[1,1]{1,0:T(1,128)} %bitcast.4.alen, s32[1,1]{1,0:T(1,128)} %bitcast.5.tlen, bf16[1,192,128]{2,1,0:T(8,128)(2,1)S(1)} %get-tuple-element.6.pick, f32[1,8,192]{2,1,0:T(8,128)S(1)} %get-tuple-element.7.stat), custom_call_target="tpu_custom_call" | custom-call | tf_op jit(solution)/shard_map/align/pallas_call | solution.py:470
Async XLA Ops:
  1.9 0.7 copy-start

commit v5 on v4

--- a/solution.py
+++ b/solution.py
@@ -284,6 +284,9 @@
         total = p * jnp.exp(pt - top) + q * jnp.exp(qt - top)
         return jnp.where(odd, total, jnp.maximum(p, q))
 
+    many = b // 2
+    span_of = lambda which: pl.ds(which[1][0], 2)
+
     def finish(n, which):
         tile = jnp.zeros((frames, 128), jnp.float32)
         for j, (d, h) in enumerate(which):
@@ -293,52 +296,64 @@
             total = jnp.sum(sm[p] * jnp.exp(best - top), 1, keepdims=True)
             for q in range(unit):
                 part = slice(q * frames, (q + 1) * frames)
-                pp[p, q // own, q % own] = acc[p, q].astype(jnp.bfloat16)
+                pp[q // own, h, d, q % own] = acc[p, q].astype(jnp.bfloat16)
                 at = 2 * (j * unit + q)
                 tile = jnp.where(lane == at, top[part], tile)
                 tile = jnp.where(lane == at + 1, total[part], tile)
         st[n] = tile.T[:tall]
-        for d, h in which:
-            p = d * half + h
-            launch(pp.at[p, 1 - side], pin.at[p], sp.at[p], rp.at[p], sibling)
-        launch(st.at[n], sin.at[n], ss.at[n], rs.at[n], sibling)
-
-    def join_sibling(n, which):
-        for d, h in which:
-            p = d * half + h
-            remote(pin.at[p], pin.at[p], sp.at[p], rp.at[p], sibling).wait_recv()
-            cs[p] = pp[p, side] + pin[p]
-            if h:
-                launch(cs.at[p], xin.at[d, h - 1], sq.at[p], rq.at[d, h - 1], across(h))
-        remote(sin.at[n], sin.at[n], ss.at[n], rs.at[n], sibling).wait_recv()
-        cst[n] = merge(st[n], sin[n])
-        h = which[0][1]
+        h, span = which[0][1], span_of(which)
+        launch(pp.at[1 - side, h, span], pin.at[h, span], sp.at[n], rp.at[n], sibling)
+        if n % many == many - 1:
+            group = pl.ds(n + 1 - many, many)
+            launch(st.at[group], sin.at[group], ss.at[h], rs.at[h], sibling)
+
+    def join_picks(n, which):
+        h, span = which[0][1], span_of(which)
+        remote(pin.at[h, span], pin.at[h, span], sp.at[n], rp.at[n], sibling).wait_recv()
+        cs[h, span] = pp[side, h, span] + pin[h, span]
         if h:
-            t = which[0][0] // 2
-            launch(cst.at[n], xst.at[t, h - 1], sv.at[n], rv.at[t, h - 1], across(h))
-
-    def join_across(n, which):
-        t = which[0][0] // 2
+            launch(cs.at[h, span], xin.at[h - 1, span], sq.at[n], rq.at[h - 1, n % many], across(h))
+
+    def join_sums(h):
+        first = (half - 1 - h) * many
+        group = pl.ds(first, many)
+        remote(st.at[group], sin.at[group], ss.at[h], rs.at[h], sibling).wait_recv()
+        for n in range(first, first + many):
+            cst[n] = merge(st[n], sin[n])
+        if h:
+            launch(cst.at[group], xst.at[h - 1], sv.at[h], rv.at[h - 1], across(h))
+
+    def across_picks(n, which):
+        span = span_of(which)
+        for h in range(1, half):
+            ref = xin.at[h - 1, span]
+            remote(ref, ref, sq.at[0], rq.at[h - 1, n % many], across(h)).wait_recv()
         for d, _ in which:
-            total = cs[d * half]
+            total = cs[0, d]
             for h in range(1, half):
-                remote(xin.at[d, h - 1], xin.at[d, h - 1], sq.at[0], rq.at[d, h - 1], across(h)).wait_recv()
-                total = total + xin[d, h - 1]
+                total = total + xin[h - 1, d]
             if d:
                 xout[d] = total
                 launch(xout.at[d], zin.at[d], sz.at[d], rz.at[d], row_peer(d))
             else:
                 zin[d] = total
-        tile = cst[n]
+
+    def across_sums():
         for h in range(1, half):
-            remote(xst.at[t, h - 1], xst.at[t, h - 1], sv.at[0], rv.at[t, h - 1], across(h)).wait_recv()
-            tile = merge(tile, xst[t, h - 1])
-        zsrc[t] = tile
-        for d, _ in which:
-            if d:
-                launch(zsrc.at[t], zst.at[d], sy.at[d], ry.at[d], row_peer(d))
-            else:
-                zst[d] = tile
+            remote(xst.at[h - 1], xst.at[h - 1], sv.at[h], rv.at[h - 1], across(h)).wait_recv()
+        for n, which in enumerate(blocks):
+            if which[0][1]:
+                continue
+            tile = cst[n]
+            for h in range(1, half):
+                tile = merge(tile, xst[h - 1, n % many])
+            t = which[1][0] // 2
+            zsrc[t] = tile
+            for d, _ in which:
+                if d:
+                    launch(zsrc.at[t], zst.at[d], sy.at[d], ry.at[d], row_peer(d))
+                else:
+                    zst[d] = tile
 
     for c in sent[: (a - 1) * (nc - 1)]:
         c.wait_send()
@@ -354,17 +369,22 @@
             pl.when(go)(remote(src, src, su.at[o, i], rf.at[o, 0], across(0)).wait_send)
             pl.when(go)(remote(tag, tag, sl.at[o, i], rl.at[o], across(0)).wait_send)
     recv_chunk(chunks - 1)
-    blocks = [[(2 * t + 1, h), (2 * t, h)] for h in reversed(range(half)) for t in reversed(range(b // 2))]
+    blocks = [[(2 * t + 1, h), (2 * t, h)] for h in reversed(range(half)) for t in reversed(range(many))]
+    last = len(blocks) - 1
     for n, which in enumerate(blocks):
         task(which, [chunks - 1])
         finish(n, which)
         if n:
-            join_sibling(n - 1, blocks[n - 1])
-    last = len(blocks) - 1
-    join_sibling(last, blocks[last])
-    for n, which in enumerate(blocks):
-        if which[0][1] == 0:
-            join_across(n, which)
+            join_picks(n - 1, blocks[n - 1])
+        if n and n % many == 0:
+            join_sums(blocks[n - 1][0][1])
+    join_picks(last, blocks[last])
+    home = [n for n in range(last + 1) if blocks[n][0][1] == 0]
+    across_picks(home[0], blocks[home[0]])
+    join_sums(0)
+    across_sums()
+    for n in home[1:]:
+        across_picks(n, blocks[n])
 
     for q in range(own):
         got = zin[0, q]
@@ -443,22 +463,22 @@
             pltpu.VMEM((pairs, rows, 128), f32),
             pltpu.VMEM((pairs, unit, frames, slots), f32),
             pltpu.VMEM((2, rows, 2 * cw), f32),
-            pltpu.VMEM((pairs, 2) + one, bf),
-            pltpu.VMEM((pairs,) + one, bf),
-            pltpu.VMEM((pairs,) + one, bf),
-            pltpu.VMEM((b, half - 1) + one, bf),
+            pltpu.VMEM((2, half, b) + one, bf),
+            pltpu.VMEM((half, b) + one, bf),
+            pltpu.VMEM((half, b) + one, bf),
+            pltpu.VMEM((half - 1, b) + one, bf),
             pltpu.VMEM((b,) + one, bf),
             pltpu.VMEM((b,) + one, bf),
             pltpu.VMEM((pairs // 2, tall, frames), f32),
             pltpu.VMEM((pairs // 2, tall, frames), f32),
             pltpu.VMEM((pairs // 2, tall, frames), f32),
-            pltpu.VMEM((b // 2, half - 1, tall, frames), f32),
+            pltpu.VMEM((half - 1, b // 2, tall, frames), f32),
             pltpu.VMEM((b // 2, tall, frames), f32),
             pltpu.VMEM((b, tall, frames), f32),
             dma((a - 1, nc)), dma((a - 1, nc)), dma((b, 2)), dma((b,)),
             dma((b, 2)), dma((b, V)), dma((b, V)),
-            dma((pairs,)), dma((pairs,)), dma((pairs // 2,)), dma((pairs // 2,)),
-            dma((pairs,)), dma((b, half - 1)), dma((pairs // 2,)), dma((b // 2, half - 1)),
+            dma((pairs // 2,)), dma((pairs // 2,)), dma((half,)), dma((half,)),
+            dma((pairs // 2,)), dma((half - 1, b // 2)), dma((half,)), dma((half - 1,)),
             dma((b,)), dma((b,)), dma((b,)), dma((b,)), dma((2 + nc,)),
         ],
         compiler_params=pltpu.CompilerParams(

time: 84.1 us -> 84.1 us (level)
  no operation moved by 1% of the time
where the time goes in v5:
time: 84.1 us; the launch traced here: 83.9 us
  Pallas kernels  81.3 us (97%)
  between operations  1.94 us (2%)
    pallas_call x1, Pallas kernels, body(): pl.pallas_call(functools.partial(emit_kernel, a, b, V), out_shape=(jax.Sh...  78.8 us
    pallas_call x1, Pallas kernels, body(): pl.pallas_call(align_kernel, out_shape=(jax.ShapeDtypeStruct(one, f32), j...  2.46 us

profile of v5, /device:TPU:0, one launch (start us, length us, event | category | flops | bytes accessed | tf_op | source)
XLA Modules:
  0.0 83.9 jit_solution(2041859417170854444)
XLA Ops:
  1.9 0.0 copy-start
  1.9 0.7 copy-done
  2.6 78.8 %emit.1 = (bf16[1,192,128]{2,1,0:T(8,128)(2,1)S(1)}, f32[1,8,192]{2,1,0:T(8,128)S(1)}) custom-call(bf16[4,192,1280]{2,1,0:T(8,128)(2,1)} %x.1, bf16[1280,1024]{1,0:T(8,128)(2,1)} %w.1, s32[4,1,128]{2,1,0:T(1,128)S(1)} %bitcast.6), custom_call_target="tpu_custom_call" | custom-call | tf_op jit(solution)/shard_map/emit/pallas_call | solution.py:453
  81.4 2.5 %align.1 = (f32[1,192,128]{2,1,0:T(8,128)}, f32[1,1]{1,0:T(1,128)}) custom-call(s32[1,1]{1,0:T(1,128)} %bitcast.4.alen, s32[1,1]{1,0:T(1,128)} %bitcast.5.tlen, bf16[1,192,128]{2,1,0:T(8,128)(2,1)S(1)} %get-tuple-element.6.pick, f32[1,8,192]{2,1,0:T(8,128)S(1)} %get-tuple-element.7.stat), custom_call_target="tpu_custom_call" | custom-call | tf_op jit(solution)/shard_map/align/pallas_call | solution.py:490
Async XLA Ops:
  1.9 0.7 copy-start
